TPU v7x, 256 devices: a 4x2x16 block of a 4x16x16 slice. The times are simulated.
256 devices in a mesh: groups: 2 (over y), expert: 128 (over z, x, core).
Axes of the slice: x: 4, y: 2, z: 16, core: 2. Of those that a mesh axis runs over, the one named last changes fastest.
The devices are a block of a 4x16x16 slice.
Arguments:
- tokens: bfloat16 [4096, 3584], P(('groups', 'expert')), parts along dimension 0, may hold values from -6 to 6
- live_counts: int32 [256], P(('groups', 'expert')), parts along dimension 0, may hold values from 8 to 16, as said below
- expert_ids: int32 [4096, 4], P(('groups', 'expert')), parts along dimension 0, may hold values from 0 to 63, all different within a row; in each aligned block of 16 rows (0 to 15, 16 to 31, ...) at most 2 rows name the same one
- gate_scores: float32 [4096, 4], P(('groups', 'expert')), parts along dimension 0, may hold values from 0.1 to 1
- gate_weight: bfloat16 [128, 3584, 512], P('expert'), may hold values from -0.09375 to 0.09375
- up_weight: bfloat16 [128, 3584, 512], P('expert'), may hold values from -0.09375 to 0.09375
- down_weight: bfloat16 [128, 512, 3584], P('expert'), may hold values from -0.1875 to 0.1875
Outputs:
- moe_out: bfloat16 [4096, 3584], P(('groups', 'expert')), parts along dimension 0
There are 2 independent parts, one for each index of `groups`. A program takes and returns all parts, laid end to end along the dimension named above; an argument that names none is the same for every part. Nothing has to cross between parts.
Inputs may be any that keep to these rules, and one draw needn't show every extreme that they name: `expert_ids`: A row names 4 different experts. In each device's aligned block of 16 rows no expert is named by more than 2 rows, a bound that some block reaches. `live_counts`: some device has all 16 slots live.
All inputs are finite; a program needn't handle non-finite values.
Results may differ from a plain program's by a relative error of at most 0.0068.
Values may be sent and summed in bfloat16 or wider, within the bound.
A program may use at most 64 MiB of HBM per device.

v0:
```python
import jax
import jax.numpy as jnp
from jax import lax
from jax.sharding import PartitionSpec as P


def partner_2(block, axis, apart):
    count = lax.axis_size(axis)
    route = []
    for low in range(count):
        high = low | 1 << apart
        if high != low and high < count:
            route += [(low, high), (high, low)]
    return lax.ppermute(block, axis, route)


def expert_rows(slot_rows, gate_weight, up_weight, down_weight):
    model_width = slot_rows.shape[-1]
    flat_rows = slot_rows.reshape(-1, model_width)
    gate_act = jnp.dot(flat_rows, gate_weight[0], preferred_element_type=jnp.float32)
    up_act = jnp.dot(flat_rows, up_weight[0], preferred_element_type=jnp.float32)
    hidden = (jax.nn.silu(gate_act) * up_act).astype(jnp.bfloat16)
    partial_value = jnp.dot(hidden, down_weight[0], preferred_element_type=jnp.float32)
    return partial_value.reshape(slot_rows.shape)


def shards(tokens, live_counts, expert_ids, gate_scores, gate_weight, up_weight, down_weight):
    tok_dev, model_width = tokens.shape
    top_count = expert_ids.shape[1]
    devices = lax.axis_size("expert")
    experts = devices // 2
    capacity = 2 * tok_dev * top_count // experts
    half_width = model_width // 2
    parity = lax.axis_index("expert") % 2
    flat_ids = expert_ids.reshape(-1)
    onehot = (flat_ids[:, None] == jnp.arange(experts, dtype=jnp.int32)[None, :]).astype(jnp.int32)
    earlier = jnp.cumsum(onehot, axis=0) - onehot
    slot_index = jnp.sum(earlier * onehot, axis=1)
    target = flat_ids * capacity + slot_index
    placing = (jnp.arange(experts * capacity, dtype=jnp.int32)[:, None] == target[None, :]).astype(
        jnp.int32
    )
    placing = (
        placing.reshape(experts * capacity, tok_dev, top_count).sum(axis=2).astype(jnp.bfloat16)
    )
    packed = jnp.dot(placing, tokens, preferred_element_type=jnp.float32).astype(jnp.bfloat16)
    outgoing = packed.reshape(devices, capacity // 2, model_width)
    slot_rows = lax.all_to_all(outgoing, "expert", split_axis=0, concat_axis=0, tiled=True)
    partner = partner_2(slot_rows, "expert", 0)
    count = slot_rows.shape[1]
    run_slot_rows = jnp.concatenate([slot_rows, partner], axis=1)
    paired = expert_rows(run_slot_rows, gate_weight, up_weight, down_weight)
    own_part = paired[:, :count]
    partner_part = paired[:, count:]
    lower_half = jnp.where(parity == 0, own_part, partner_part)
    second = jnp.where(parity == 0, partner_part, own_part)
    stacked = jnp.stack([lower_half, second], axis=1)
    partial_value = stacked.reshape(devices, capacity, model_width)
    partner_sum = partner_2(partial_value.astype(jnp.bfloat16), "expert", 0).astype(
        partial_value.dtype
    )
    summed = partial_value + partner_sum
    own_part = lax.dynamic_slice_in_dim(summed, parity * half_width, half_width, 2).astype(
        jnp.bfloat16
    )
    returned = lax.all_to_all(own_part, "expert", split_axis=0, concat_axis=0, tiled=True)
    returned = returned.reshape(experts, 2, capacity, half_width)
    picked = returned[flat_ids, :, slot_index, :]
    picked = picked.reshape(tok_dev, top_count, model_width).astype(jnp.float32)
    weighted = jnp.sum(picked * gate_scores[:, :, None], axis=1)
    live_mask = jnp.arange(tok_dev, dtype=jnp.int32) < live_counts[0]
    return jnp.where(live_mask[:, None], weighted, jnp.zeros_like(weighted)).astype(jnp.bfloat16)


def solution(mesh):
    in_specs = (
        P(("groups", "expert"), None),
        P(("groups", "expert")),
        P(("groups", "expert"), None),
        P(("groups", "expert"), None),
        P("expert", None, None),
        P("expert", None, None),
        P("expert", None, None),
    )
    out_specs = P(("groups", "expert"), None)
    return jax.shard_map(shards, mesh=mesh, in_specs=in_specs, out_specs=out_specs, check_vma=False)
```

profile of v0, /device:TPU:33, one launch (start us, length us, event | category | flops | bytes accessed | tf_op | source)
XLA Modules:
  0.0 175.5 jit_solution(17304223445592291516)
XLA Ops:
  0.0 0.0 copy-start
  0.0 0.8 copy.62
  0.8 0.1 eq.37
  0.9 0.1 fusion.9
  1.0 0.1 reduce_window_sum.11
  1.1 0.2 select_reduce_fusion
  1.2 0.1 reduce_sum.32
  1.3 0.1 copy.63
  1.4 0.7 multiply_add_fusion
  2.1 0.1 convert_reduce_fusion
  2.2 0.0 copy-done
  2.2 0.4 fusion
  2.6 0.5 broadcast.80
  3.1 1.3 reduce
  4.5 0.2 reshape.97
  4.7 76.5 %all_to_all.10 = bf16[128,2,1792]{2,1,0:T(2,128)(2,1)S(1)} all-to-all(bf16[128,2,1792]{2,1,0:T(2,128)(2,1)S(1)} %reshape.97), channel_id=1, replica_groups=mesh['groups'=2,'expert'=128] {'expert'}, dimensions={0} | all-to-all | bytes 1835008 | tf_op jit(solution)/shard_map/all_to_all | solution.py:48
  81.2 0.7 reshape.98
  81.9 1.0 copy.65
  83.0 2.3 %collective-permute-start = (bf16[128,1,3584]{2,0,1:T(8,128)(2,1)}, bf16[128,1,3584]{2,0,1:T(8,128)(2,1)S(1)}, u32[]{:S(2)}, u32[]{:S(2)}) collective-permute-start(bf16[128,1,3584]{2,0,1:T(8,128)(2,1)} %copy.65), channel_id=1, source_target_pairs={{0,1},{1,0},{2,3},{3,2},{4,5},{5,4},{6,7},{7,6},{8,9},{9,8},{10,11... | collective-permute-start | bytes 2752520 | tf_op jit(solution)/shard_map/ppermute | solution.py:14
  85.2 2.3 %collective-permute-done = bf16[128,1,3584]{2,0,1:T(8,128)(2,1)S(1)} collective-permute-done((bf16[128,1,3584]{2,0,1:T(8,128)(2,1)}, bf16[128,1,3584]{2,0,1:T(8,128)(2,1)S(1)}, u32[]{:S(2)}, u32[]{:S(2)}) %collective-permute-start) | collective-permute-done | bytes 917536 | tf_op jit(solution)/shard_map/ppermute | solution.py:14
  87.5 1.4 copy.66
  88.9 5.4 %pad_maximum_fusion = bf16[128,2,3584]{2,1,0:T(2,128)(2,1)} fusion(bf16[128,1,3584]{2,1,0:T(2,128)(2,1)S(1)} %copy.66, bf16[128,1,3584]{2,1,0:T(2,128)(2,1)S(1)} %reshape.98), kind=kLoop, calls=%fused_computation.12 | loop fusion | flops 3670016 | bytes 3670016 | tf_op jit(solution)/shard_map/concatenate | solution.py:51
  94.3 4.1 %reshape.85 = bf16[256,3584]{1,0:T(8,128)(2,1)S(1)} reshape(bf16[128,2,3584]{2,1,0:T(2,128)(2,1)} %pad_maximum_fusion) | data formatting | bytes 3670016 | tf_op jit(solution)/shard_map/reshape | solution.py:19
  98.4 0.0 copy-start.3
  98.4 3.3 %fusion.5 = f32[256,512]{1,0:T(8,128)S(1)} fusion(bf16[256,3584]{1,0:T(8,128)(2,1)S(1)} %reshape.85, bf16[1,3584,512]{2,1,0:T(8,128)(2,1)} %param.11), kind=kOutput, calls=%fused_computation.8 | convolution fusion | flops 939524096 | bytes 6029312 | tf_op jit(solution)/shard_map/dot_general | solution.py:20
  101.7 0.0 copy-done.3
  101.7 1.1 multiply_convert_fusion
  102.9 0.1 dot_general.17
  103.0 3.2 %fusion.1 = f32[128,2,3584]{2,0,1:T(8,128)S(1)} fusion(bf16[1,512,3584]{2,1,0:T(8,128)(2,1)} %param.13, bf16[128,2,512]{2,1,0:T(2,128)(2,1)S(1)} %dot_general.17), kind=kOutput, calls=%fused_computation.4 | convolution fusion | flops 939524096 | bytes 7602176 | tf_op jit(solution)/shard_map/dot_general | solution.py:23
  106.1 0.3 select_bitcast_fusion.1
  106.4 0.0 copy-start.1
  106.4 1.7 fusion.17
  108.2 0.0 copy-done.1
  108.2 0.4 collective-permute-start.1
  108.6 2.0 %maximum_bitcast_fusion = f32[128,2,3584]{2,0,1:T(8,128)S(1)} fusion(f32[128,1,1,3584]{3,0,2,1:T(8,128)} %copy-done.1, f32[128,1,1,3584]{3,0,2,1:T(8,128)S(1)} %get-tuple-element.5), kind=kLoop, calls=%fused_computation.3 | loop fusion | flops 917504 | bytes 7340032 | tf_op jit(solution)/shard_map/reshape | solution.py:58
  110.6 1.8 %collective-permute-done.1 = bf16[128,2,3584]{2,0,1:T(8,128)(2,1)} collective-permute-done((bf16[128,2,3584]{2,0,1:T(8,128)(2,1)}, bf16[128,2,3584]{2,0,1:T(8,128)(2,1)}, u32[]{:S(2)}, u32[]{:S(2)}) %collective-permute-start.1) | collective-permute-done | bytes 1835040 | tf_op jit(solution)/shard_map/ppermute | solution.py:14
  112.4 1.4 fusion.7
  113.8 0.0 copy-start.2
  113.8 1.9 %copy.68 = bf16[128,2,1792]{2,1,0:T(2,128)(2,1)} copy(bf16[128,2,1792]{2,0,1:T(8,128)(2,1)S(1)} %fusion.7) | data formatting | bytes 1835008 | tf_op jit(solution)/shard_map/convert_element_type | solution.py:63
  115.7 10.0 %all-to-all-start.1 = ((bf16[128,2,1792]{2,1,0:T(2,128)(2,1)}), bf16[128,2,1792]{2,1,0:T(2,128)(2,1)S(1)}, u32[]{:S(2)}, u32[]{:S(2)}) async-start(bf16[128,2,1792]{2,1,0:T(2,128)(2,1)} %copy.68), calls=%async_computation.1 | async-start | bytes 1835008 | tf_op jit(solution)/shard_map/all_to_all | solution.py:66
  125.7 0.1 reshape.88
  125.8 0.0 copy-done.2
  125.8 0.1 copy.71
  126.6 44.8 %all-to-all-done.1 = bf16[128,2,1792]{2,1,0:T(2,128)(2,1)S(1)} async-done(((bf16[128,2,1792]{2,1,0:T(2,128)(2,1)}), bf16[128,2,1792]{2,1,0:T(2,128)(2,1)S(1)}, u32[]{:S(2)}, u32[]{:S(2)}) %all-to-all-start.1) | async-done | bytes 917536 | tf_op jit(solution)/shard_map/all_to_all | solution.py:66
  171.4 0.7 copy.70
  172.1 1.5 gather_fusion
  173.7 0.4 reshape.89
  174.1 0.6 multiply_reduce_fusion
  174.8 0.7 select_convert_fusion
  (2 shorter events, 0.0 us)
Async XLA Ops:
  0.0 2.2 %copy-start = (bf16[16,3584]{1,0:T(8,128)(2,1)S(1)}, bf16[16,3584]{1,0:T(8,128)(2,1)}, u32[]{:S(2)}) copy-start(bf16[16,3584]{1,0:T(8,128)(2,1)} %param.7) | copy-start | bytes 344068
  83.0 4.6 %collective-permute-start = (bf16[128,1,3584]{2,0,1:T(8,128)(2,1)}, bf16[128,1,3584]{2,0,1:T(8,128)(2,1)S(1)}, u32[]{:S(2)}, u32[]{:S(2)}) collective-permute-start(bf16[128,1,3584]{2,0,1:T(8,128)(2,1)} %copy.65), channel_id=1, source_target_pairs={{0,1},{1,0},{2,3},{3,2},{4,5},{5,4},{6,7},{7,6},{8,9},{9,8},{10,11... | collective-permute-start | bytes 2752520 | tf_op jit(solution)/shard_map/ppermute | solution.py:14
  98.4 3.3 %copy-start.3 = (bf16[1,3584,512]{2,1,0:T(8,128)(2,1)S(1)}, bf16[1,3584,512]{2,1,0:T(8,128)(2,1)}, u32[]{:S(2)}) copy-start(bf16[1,3584,512]{2,1,0:T(8,128)(2,1)} %param.12) | copy-start | bytes 11010052
  106.4 1.8 %copy-start.1 = (f32[128,1,1,3584]{3,0,2,1:T(8,128)}, f32[128,1,1,3584]{3,0,2,1:T(8,128)S(1)}, u32[]{:S(2)}) copy-start(f32[128,1,1,3584]{3,0,2,1:T(8,128)S(1)} %get-tuple-element.6) | copy-start | bytes 5505028
  108.2 4.1 %collective-permute-start.1 = (bf16[128,2,3584]{2,0,1:T(8,128)(2,1)}, bf16[128,2,3584]{2,0,1:T(8,128)(2,1)}, u32[]{:S(2)}, u32[]{:S(2)}) collective-permute-start(bf16[128,2,3584]{2,0,1:T(8,128)(2,1)} %fusion.17), channel_id=1, source_target_pairs={{0,1},{1,0},{2,3},{3,2},{4,5},{5,4},{6,7},{7,6},{8,9},{9,8},{10,11... | collective-permute-start | bytes 5505032 | tf_op jit(solution)/shard_map/ppermute | solution.py:14
  113.8 12.0 %copy-start.2 = (f32[16,4]{0,1:T(4,128)S(1)}, f32[16,4]{0,1:T(4,128)}, u32[]{:S(2)}) copy-start(f32[16,4]{0,1:T(4,128)} %param.10) | copy-start | bytes 772
  115.7 55.8 %all-to-all-start.1 = ((bf16[128,2,1792]{2,1,0:T(2,128)(2,1)}), bf16[128,2,1792]{2,1,0:T(2,128)(2,1)S(1)}, u32[]{:S(2)}, u32[]{:S(2)}) async-start(bf16[128,2,1792]{2,1,0:T(2,128)(2,1)} %copy.68), calls=%async_computation.1 | async-start | bytes 1835008 | tf_op jit(solution)/shard_map/all_to_all | solution.py:66
where the time goes:
time: 177 us; the launch traced here: 175 us
  blocking collectives  76.5 us (43%)
  waiting for transfers between devices  48.9 us (28%)
  other arithmetic  14.7 us (8%)
  local copies, waits for them, and re-layouts  13.9 us (8%)
  starting transfers between devices  12.7 us (7%)
  matrix products  7.99 us (5%)
    all_to_all x1, blocking collectives, shards(): lax.all_to_all(outgoing, 'expert', split_axis=0, concat_axis=0, tiled=True)  76.5 us
    all_to_all x1, waiting for transfers between devices, shards(): lax.all_to_all(own_part, 'expert', split_axis=0, concat_axis=0, tiled=True)  44.8 us
    all_to_all x1, starting transfers between devices, shards(): lax.all_to_all(own_part, 'expert', split_axis=0, concat_axis=0, tiled=True)  10 us
    concatenate x1, other arithmetic, shards(): run_slot_rows = jnp.concatenate([slot_rows, partner], axis=1)  5.41 us
    ppermute x2, waiting for transfers between devices, partner_2(): return lax.ppermute(block, axis, route)  4.09 us
    reshape x1, local copies, waits for them, and re-layouts, expert_rows(): flat_rows = slot_rows.reshape(-1, model_width)  4.06 us
  transfers between devices with their start and end apart: 3, of which 3 were waited for; matrix products, arithmetic and copies ran while one was open for 1% of the time, Pallas kernels for 0%

commit v1 on v0

v1 whole, which is shorter than its diff:
```python
import functools

import jax
import jax.numpy as jnp
from jax import lax
from jax.experimental import pallas as pl
from jax.experimental.pallas import tpu as pltpu
from jax.sharding import PartitionSpec as P

MESH = pl.DeviceIdType.MESH
X_CHIPS = 4
CORES = 2
SLOTS = 2
PIECES = 7
PER_ROUND = 4
LANES = 128
F32 = jnp.float32
BF16 = jnp.bfloat16


def routing(ids_ref, scores_ref, live, tok_dev):
    top = ids_ref.shape[0]
    lane = lax.broadcasted_iota(jnp.int32, (tok_dev, LANES), 1)
    token = lax.broadcasted_iota(jnp.int32, (tok_dev, LANES), 0)
    row = lax.broadcasted_iota(jnp.int32, (tok_dev, tok_dev), 0)
    col = lax.broadcasted_iota(jnp.int32, (tok_dev, tok_dev), 1)
    ids = ids_ref[...].astype(F32)
    scores = scores_ref[...]
    expert = lax.div(lane, SLOTS).astype(F32)
    chosen = jnp.zeros((tok_dev, LANES), F32)
    weight = jnp.zeros((tok_dev, LANES), F32)
    for k in range(top):
        id_k = jnp.sum(jnp.where(row == col, ids[k : k + 1, :], 0.0), axis=1, keepdims=True)
        score_k = jnp.sum(jnp.where(row == col, scores[k : k + 1, :], 0.0), axis=1, keepdims=True)
        hit = expert == id_k
        chosen = jnp.where(hit, 1.0, chosen)
        weight = jnp.where(hit, score_k, weight)
    earlier = jnp.where(col < row, 1.0, 0.0).astype(BF16)
    rank = jnp.dot(earlier, chosen.astype(BF16), preferred_element_type=F32)
    mine = (rank == lax.rem(lane, SLOTS).astype(F32)) & (token < live)
    return jnp.where(mine, weight, 0.0)


def kernel(
    planes,
    tokens_ref, live_ref, ids_ref, scores_ref, gate_ref, up_ref, down_ref,
    out_ref,
    head, tail, xout, xin, hidden, yout, yin, contrib, rs_in, rs_out, wg, wu, wd,
    load_sem, w_sem, w_send, w_recv, ag_send, ag_recv, x_send, x_recv, y_send, y_recv,
    rs_send, rs_recv,
):
    tok_dev, width = tokens_ref.shape
    ff_half = gate_ref.shape[2]
    piece = width // PIECES
    half = planes // 2
    cut = (PIECES + 1) // 2
    block = PER_ROUND * SLOTS
    rounds = planes // PER_ROUND
    order = [0]
    for d in range(1, half):
        order += [d, planes - d]
    order.append(half)

    me = lax.axis_index("expert")
    core = lax.rem(me, CORES)
    x = lax.rem(lax.div(me, CORES), X_CHIPS)
    z = lax.div(me, CORES * X_CHIPS)

    def at(z_of, x_of):
        return (z_of * X_CHIPS + x_of) * CORES + core

    above = at(lax.rem(z + 1, planes), x)
    below = at(lax.rem(z + planes - 1, planes), x)
    other = me + 1 - 2 * core
    ahead = [at(z, lax.rem(x + dx, X_CHIPS)) for dx in range(X_CHIPS)]
    behind = [at(z, lax.rem(x + X_CHIPS - dx, X_CHIPS)) for dx in range(X_CHIPS)]

    def remote(src, dst, send, recv, device):
        return pltpu.make_async_remote_copy(
            src_ref=src, dst_ref=dst, send_sem=send, recv_sem=recv,
            device_id={"expert": device}, device_id_type=MESH,
        )

    barrier = pltpu.get_barrier_semaphore()
    peers = [above, below, other] + ahead[1:]
    for peer in peers:
        pl.semaphore_signal(barrier, inc=1, device_id={"expert": peer}, device_id_type=MESH)

    loads = [
        pltpu.make_async_copy(
            tokens_ref.at[:, pl.ds(0, piece)], head.at[0, :, pl.ds(2 * LANES, piece)], load_sem.at[0]
        )
    ]
    for k in range(1, PIECES):
        loads.append(
            pltpu.make_async_copy(
                tokens_ref.at[:, pl.ds(k * piece, piece)], tail.at[0, k - 1], load_sem.at[k]
            )
        )
    for load in loads:
        load.start()
    weights = [(gate_ref, wg), (up_ref, wu), (down_ref, wd)]
    own_weights = [
        pltpu.make_async_copy(src.at[0], dst.at[0], w_sem.at[i]) for i, (src, dst) in enumerate(weights)
    ]
    other_weights = [
        remote(src.at[0], dst.at[1], w_send.at[i], w_recv.at[i], other)
        for i, (src, dst) in enumerate(weights)
    ]
    table = routing(ids_ref, scores_ref, live_ref[0], tok_dev)
    table_high = table.astype(BF16)
    head[0, :, 0:LANES] = table_high
    head[0, :, LANES : 2 * LANES] = (table - table_high.astype(F32)).astype(BF16)

    def chunk(q, k):
        return head.at[q] if isinstance(k, int) and k == 0 else tail.at[q, k - 1]

    def pass_up(q, k):
        return remote(chunk(q, k), chunk(q + 1, k), ag_send.at[q, k], ag_recv.at[q + 1, k], above)

    def pass_down(q, k):
        at_q = half if q == 0 else q
        to = planes - 1 if q == 0 else q - 1
        return remote(chunk(q, k), chunk(to, k), ag_send.at[at_q, k], ag_recv.at[to, k], below)

    def take(q, k):
        remote(chunk(q, k), chunk(q, k), ag_send.at[q, k], ag_recv.at[q, k], above).wait_recv()

    pl.semaphore_wait(barrier, len(peers))
    for k in range(PIECES):
        loads[k].wait()
        pass_up(0, k).start()
        pass_down(0, k).start()
    for i in range(len(weights)):
        other_weights[i].start()
        own_weights[i].start()

    rows = X_CHIPS * block
    lane_of = lax.broadcasted_iota(jnp.int32, (LANES, rows), 0)
    row_of = lax.broadcasted_iota(jnp.int32, (LANES, rows), 1)
    chip_of = lax.rem(x + lax.div(row_of, block), X_CHIPS)
    wanted = (z * X_CHIPS + chip_of) * SLOTS + lax.rem(row_of, SLOTS)
    select = jnp.where(lane_of == wanted, 1.0, 0.0).astype(BF16)
    flat = PER_ROUND * tok_dev
    plane_a = lax.div(lax.broadcasted_iota(jnp.int32, (flat, rows), 0), tok_dev)
    plane_b = lax.rem(lax.div(lax.broadcasted_iota(jnp.int32, (flat, rows), 1), SLOTS), PER_ROUND)
    same_plane = plane_a == plane_b

    def of_round(r):
        return order[r * PER_ROUND : (r + 1) * PER_ROUND]

    def picked(r, low):
        part = jnp.concatenate([head[q, :, low * LANES : (low + 1) * LANES] for q in of_round(r)], axis=0)
        return part

    def x_copy(r, dx):
        return remote(
            xout.at[r, dx - 1], xin.at[r * X_CHIPS + dx], x_send.at[r, dx - 1], x_recv.at[r, dx - 1],
            ahead[dx],
        )

    def pack(r):
        used = jnp.where(picked(r, 0).astype(F32) != 0.0, 1.0, 0.0).astype(BF16)
        place = jnp.dot(used, select, preferred_element_type=F32)
        place = jnp.where(same_plane, place, 0.0).astype(BF16)
        for k in range(PIECES):
            if k == 0:
                parts = [head[q, :, 2 * LANES :] for q in of_round(r)]
            else:
                parts = [tail[q, k - 1] for q in of_round(r)]
            packed = lax.dot_general(
                place, jnp.concatenate(parts, axis=0), (((0,), (0,)), ((), ())),
                preferred_element_type=F32,
            )
            cols = slice(k * piece, (k + 1) * piece)
            xin[r * X_CHIPS, :, cols] = packed[0:block].astype(BF16)
            for dx in range(1, X_CHIPS):
                xout[r, dx - 1, :, cols] = packed[dx * block : (dx + 1) * block].astype(BF16)
        for dx in range(1, X_CHIPS):
            x_copy(r, dx).start()

    packed_rounds = 0
    for d in range(1, half):
        up_q, down_q = d, planes - d
        if d + 1 < half:
            take(up_q, 0)
            pass_up(up_q, 0).start()
            take(down_q, 0)
            pass_down(down_q, 0).start()

            @pl.loop(1, PIECES)
            def _(k):
                take(up_q, k)
                pass_up(up_q, k).start()
                take(down_q, k)
                pass_down(down_q, k).start()
        else:
            for k in range(PIECES):
                take(up_q, k)
                if k < cut:
                    pass_up(up_q, k).start()
                take(down_q, k)
                if k >= cut:
                    pass_down(down_q, k).start()
        while packed_rounds < rounds - 1 and all(
            min(q, planes - q) <= d for q in of_round(packed_rounds)
        ):
            pack(packed_rounds)
            packed_rounds += 1
    for k in range(PIECES):
        take(half, k)
    for r in range(packed_rounds, rounds):
        pack(r)

    for copy in own_weights:
        copy.wait()
    for copy in other_weights:
        copy.wait_recv()
    for r in range(rounds):
        for dx in range(1, X_CHIPS):
            x_copy(r, dx).wait_recv()

    n_rows = rounds * rows
    step = min(256, ff_half)

    for part in range(CORES):

        @pl.loop(0, ff_half // step)
        def _(i):
            cols = pl.ds(pl.multiple_of(i * step, step), step)
            inputs = xin[...].reshape(n_rows, width)
            gate = jnp.dot(inputs, wg[part, :, cols], preferred_element_type=F32)
            up = jnp.dot(inputs, wu[part, :, cols], preferred_element_type=F32)
            hidden[part, :, cols] = (gate / (1.0 + jnp.exp(-gate)) * up).astype(BF16)

    last = rounds - 1

    def y_piece(dx, k):
        cols = pl.ds(k * piece, piece)
        slot = last * X_CHIPS + dx
        return remote(
            yout.at[slot, :, cols], yin.at[slot, :, cols], y_send.at[last + dx - 1, k],
            y_recv.at[last + dx - 1, k], behind[dx],
        )

    def y_copy(r, dx):
        slot = r * X_CHIPS + dx
        return remote(
            yout.at[slot], yin.at[slot], y_send.at[r, dx - 1], y_recv.at[r, dx - 1], behind[dx]
        )

    for k in range(PIECES):
        cols = slice(k * piece, (k + 1) * piece)
        result = jnp.dot(hidden[0], wd[0, :, cols], preferred_element_type=F32)
        result += jnp.dot(hidden[1], wd[1, :, cols], preferred_element_type=F32)
        result = result.reshape(rounds, X_CHIPS, block, piece).astype(BF16)
        for r in range(rounds):
            yin[r * X_CHIPS, :, cols] = result[r, 0]
            for dx in range(1, X_CHIPS):
                yout[r * X_CHIPS + dx, :, cols] = result[r, dx]
        for dx in range(1, X_CHIPS):
            y_piece(dx, k).start()
    for r in range(last - 1, -1, -1):
        for dx in range(1, X_CHIPS):
            y_copy(r, dx).start()

    def weights_of(r, low):
        part = jnp.dot(picked(r, low), select, preferred_element_type=F32)
        return jnp.where(same_plane, part, 0.0).astype(BF16)

    def combine(r, k, high, low):
        cols = slice(k * piece, (k + 1) * piece)
        rows_in = yin[r * X_CHIPS : (r + 1) * X_CHIPS, :, cols].reshape(rows, piece)
        total = jnp.dot(high, rows_in, preferred_element_type=F32)
        total += jnp.dot(low, rows_in, preferred_element_type=F32)
        for j, q in enumerate(of_round(r)):
            contrib[q, k] = total[j * tok_dev : (j + 1) * tok_dev]

    def rs_down(q, k):
        return remote(rs_out.at[q, k], rs_in.at[q - 1, k], rs_send.at[q, k], rs_recv.at[q - 1, k], below)

    def rs_up(q, k):
        return remote(rs_out.at[q, k], rs_in.at[q + 1, k], rs_send.at[q, k], rs_recv.at[q + 1, k], above)

    def rs_take(q, k):
        remote(rs_in.at[q, k], rs_in.at[q, k], rs_recv.at[q, k], rs_recv.at[q, k], above).wait_recv()

    high, low = weights_of(last, 0), weights_of(last, 1)
    for k in range(PIECES):
        for dx in range(1, X_CHIPS):
            y_piece(dx, k).wait_recv()
        combine(last, k, high, low)
        rs_out[half, k] = contrib[half, k].astype(BF16)
        (rs_down if k < cut else rs_up)(half, k).start()

    combined = {last}
    for d in range(half - 1, 0, -1):
        down_q, up_q = d, planes - d
        for q in (down_q, up_q):
            r = order.index(q) // PER_ROUND
            if r not in combined:
                combined.add(r)
                for dx in range(1, X_CHIPS):
                    y_copy(r, dx).wait_recv()
                high, low = weights_of(r, 0), weights_of(r, 1)
                for k in range(PIECES):
                    combine(r, k, high, low)
        if d == half - 1:
            for k in range(PIECES):
                for q, incoming, push in ((down_q, k < cut, rs_down), (up_q, k >= cut, rs_up)):
                    if incoming:
                        rs_take(q, k)
                        rs_out[q, k] = (contrib[q, k] + rs_in[q, k].astype(F32)).astype(BF16)
                    else:
                        rs_out[q, k] = contrib[q, k].astype(BF16)
                    push(q, k).start()
        else:

            @pl.loop(0, PIECES)
            def _(k):
                for q, push in ((down_q, rs_down), (up_q, rs_up)):
                    rs_take(q, k)
                    rs_out[q, k] = (contrib[q, k] + rs_in[q, k].astype(F32)).astype(BF16)
                    push(q, k).start()

    r = 0
    if r not in combined:
        for dx in range(1, X_CHIPS):
            y_copy(r, dx).wait_recv()
        high, low = weights_of(r, 0), weights_of(r, 1)
        for k in range(PIECES):
            combine(r, k, high, low)
    for k in range(PIECES):
        rs_take(0, k)
        rs_take(planes, k)
        total = contrib[0, k] + rs_in[0, k].astype(F32) + rs_in[planes, k].astype(F32)
        out_ref[:, k * piece : (k + 1) * piece] = total.astype(BF16)

    for copy in other_weights:
        copy.wait_send()
    for k in range(PIECES):
        pass_up(0, k).wait_send()
        pass_down(0, k).wait_send()
    for d in range(1, half):
        for k in range(PIECES):
            if d + 1 < half or k < cut:
                pass_up(d, k).wait_send()
            if d + 1 < half or k >= cut:
                pass_down(planes - d, k).wait_send()
    for r in range(rounds):
        for dx in range(1, X_CHIPS):
            x_copy(r, dx).wait_send()
            if r < last:
                y_copy(r, dx).wait_send()
    for k in range(PIECES):
        for dx in range(1, X_CHIPS):
            y_piece(dx, k).wait_send()
        (rs_down if k < cut else rs_up)(half, k).wait_send()
        for d in range(1, half):
            rs_down(d, k).wait_send()
            rs_up(planes - d, k).wait_send()


def shards(tokens, live_counts, expert_ids, gate_scores, gate_weight, up_weight, down_weight):
    tok_dev, width = tokens.shape
    ff_half = gate_weight.shape[2]
    planes = lax.axis_size("expert") // (X_CHIPS * CORES)
    rounds = planes // PER_ROUND
    piece = width // PIECES
    block = PER_ROUND * SLOTS
    slots = rounds * X_CHIPS
    vmem, dma = pltpu.VMEM, pltpu.SemaphoreType.DMA
    scratch = [
        vmem((planes, tok_dev, 2 * LANES + piece), BF16),
        vmem((planes, PIECES - 1, tok_dev, piece), BF16),
        vmem((rounds, X_CHIPS - 1, block, width), BF16),
        vmem((slots, block, width), BF16),
        vmem((CORES, slots * block, ff_half), BF16),
        vmem((slots, block, width), BF16),
        vmem((slots, block, width), BF16),
        vmem((planes, PIECES, tok_dev, piece), F32),
        vmem((planes + 1, PIECES, tok_dev, piece), BF16),
        vmem((planes, PIECES, tok_dev, piece), BF16),
        vmem((CORES, width, ff_half), BF16),
        vmem((CORES, width, ff_half), BF16),
        vmem((CORES, ff_half, width), BF16),
        dma((PIECES,)),
        dma((3,)),
        dma((3,)),
        dma((3,)),
        dma((planes, PIECES)),
        dma((planes, PIECES)),
        dma((rounds, X_CHIPS - 1)),
        dma((rounds, X_CHIPS - 1)),
        dma((rounds + X_CHIPS - 2, PIECES)),
        dma((rounds + X_CHIPS - 2, PIECES)),
        dma((planes, PIECES)),
        dma((planes + 1, PIECES)),
    ]
    in_vmem = pl.BlockSpec(memory_space=pltpu.VMEM)
    in_smem = pl.BlockSpec(memory_space=pltpu.SMEM)
    anywhere = pl.BlockSpec(memory_space=pl.ANY)
    return pl.pallas_call(
        functools.partial(kernel, planes),
        out_shape=jax.ShapeDtypeStruct((tok_dev, width), BF16),
        in_specs=[anywhere, in_smem, in_vmem, in_vmem, anywhere, anywhere, anywhere],
        out_specs=in_vmem,
        scratch_shapes=scratch,
        compiler_params=pltpu.CompilerParams(
            collective_id=0, has_side_effects=True, vmem_limit_bytes=60 * 1024 * 1024
        ),
        name="moe_layer",
    )(tokens, live_counts, expert_ids.T, gate_scores.T, gate_weight, up_weight, down_weight)


def solution(mesh):
    both = P(("groups", "expert"), None)
    weight = P("expert", None, None)
    in_specs = (both, P(("groups", "expert")), both, both, weight, weight, weight)
    return jax.shard_map(shards, mesh=mesh, in_specs=in_specs, out_specs=both, check_vma=False)
```

time: 177 us -> 102 us (0.58)
  the two profiles are of different devices: /device:TPU:33 before, /device:TPU:40 now
where the time goes in v1:
time: 102 us
  Pallas kernels  99.3 us (97%)
  local copies, waits for them, and re-layouts  1.55 us (2%)
    pallas_call x1, Pallas kernels, shards(): pl.pallas_call(functools.partial(kernel, planes), out_shape=jax.ShapeDtyp...  99.3 us

profile of v1, /device:TPU:40, one launch (start us, length us, event | category | flops | bytes accessed | tf_op | source)
XLA Modules:
  0.0 101.5 jit_solution(5890886456956846678)
XLA Ops:
  0.7 99.3 %moe_layer.1 = bf16[16,3584]{1,0:T(8,128)(2,1)} custom-call(bf16[16,3584]{1,0:T(8,128)(2,1)} %tokens_ref.1, s32[1]{0:T(128)S(6)} %copy.9.live_ref, s32[4,16]{1,0:T(4,128)} %bitcast.2, f32[4,16]{1,0:T(4,128)} %bitcast.3, bf16[1,3584,512]{2,1,0:T(8,128)(2,1)} %gate_ref.1, bf16[1,3584,512]{2,1,0:T(8,128)(2,1)} %up_ref.1, bf16[1,512,3584]{2,1,0:T(8,128)(2,1)} %down_ref.1), custom_call_target="tpu_custom_call" | custom-call | tf_op jit(solution)/shard_map/moe_layer/pallas_call | solution.py:403
  100.0 1.6 %copy.10 = bf16[16,3584]{1,0:T(8,128)(2,1)} copy(bf16[16,3584]{1,0:T(8,128)(2,1)} %moe_layer.1) | data formatting | bytes 229376
